TPU v7x, 32 devices: a whole 2x2x4 slice. The times are simulated.
32 devices in a mesh: gx: 4 (over y, x), gy: 2 (over core), gz: 4 (over z).
Axes of the slice: x: 2, y: 2, z: 4, core: 2. Of those that a mesh axis runs over, the one named last changes fastest.
Arguments:
- params: float32 [12, 7168, 1536], P('gx', 'gy', 'gz'), may hold values from -100 to 100
- grads: bfloat16 [12, 7168, 1536], P('gx', 'gy', 'gz'), may hold values from -300 to 300
- row_state: float32 [12, 7168], P('gx', 'gy'), may hold values from 0.01 to 1
- col_state: float32 [12, 1536], P('gx', 'gz'), may hold values from 0.01 to 1
Outputs:
- new_params: float32 [12, 7168, 1536], P('gx', 'gy', 'gz')
- row_new: float32 [12, 7168], P('gx', 'gy')
- col_new: float32 [12, 1536], P('gx', 'gz')
- applied_step: float32 [12, 7168, 1536], P('gx', 'gy', 'gz')
- compute_copy: bfloat16 [12, 7168, 1536], P('gx', 'gy')
All inputs are finite; a program needn't handle non-finite values.
Results may differ from a plain program's by a relative error of at most 0.0004.
Values may be sent and summed in bfloat16 or wider, within the bound.
A program may use at most 192 MiB of HBM per device.

v0:
```python
import functools
import jax
import jax.numpy as jnp
from jax import lax
from jax.experimental import pallas as pl
from jax.experimental.pallas import tpu as pltpu
from jax.sharding import PartitionSpec as P

decay_rate = 0.842
tiny_term = 1e-30
step_share = 0.01
clip_limit = 1.0
LANES = 128
f32, bf16 = jnp.float32, jnp.bfloat16


def fold(values):
    return jnp.sum(values.reshape(values.shape[0] // 8, 8, values.shape[1]), axis=0)


def fold_lanes(row):
    return sum(row[:, i : i + LANES] for i in range(0, row.shape[1], LANES))


def split(values):
    high = values.astype(bf16)
    return high, (values - high.astype(f32)).astype(bf16)


def row_dots(left, values):
    dims = (((1,), (1,)), ((), ()))
    high, low = split(values)
    return lax.dot_general(left, high, dims, preferred_element_type=f32) + lax.dot_general(
        left, low, dims, preferred_element_type=f32
    )


def exchange(axis, bufs, send, recv):
    n, me = lax.axis_size(axis), lax.axis_index(axis)
    copies = []
    for i, buf in enumerate(bufs):
        for d in range(1, n):
            slot = i * (n - 1) + d - 1
            copy = pltpu.make_async_remote_copy(
                src_ref=buf.at[me],
                dst_ref=buf.at[me],
                send_sem=send.at[slot],
                recv_sem=recv.at[slot],
                device_id={axis: lax.rem(me + d, n)},
                device_id_type=pl.DeviceIdType.MESH,
            )
            copy.start()
            copies.append(copy)
    return copies


def finish(copies):
    for copy in copies:
        copy.wait()


def total(buf):
    return functools.reduce(lambda a, b: a + b, [buf[i] for i in range(buf.shape[0])])


def stats_kernel(
    layers, chunk, small,
    p_hbm, g_hbm, row_ref, col_ref,
    row_out, col_out, rr_out, rc_out, big_hbm, small_hbm,
    p_vm, g_vm, new_vm, row_all, col_all, sc_z, sc_y, up_z, up_y, up_x,
    p_sem, g_sem, o_sem,
    rz_s, rz_r, cy_s, cy_r, sy_s, sy_r, uz_s, uz_r, uy_s, uy_r, ux_s, ux_r,
):
    rows_total, columns = g_vm.shape
    rows = rows_total // layers
    nb, per, chunks = rows // LANES, chunk // LANES, rows // chunk
    nx, ny, nz = (lax.axis_size(a) for a in ("gx", "gy", "gz"))
    me_x, me_y, me_z = (lax.axis_index(a) for a in ("gx", "gy", "gz"))
    rows_all, columns_all = rows * ny, columns * nz

    loads = []
    for k in range(layers * chunks):
        part = pl.ds(k * chunk, chunk)
        g_copy = pltpu.make_async_copy(g_hbm.at[part], g_vm.at[part], g_sem.at[k])
        p_copy = pltpu.make_async_copy(p_hbm.at[part], p_vm.at[part], p_sem.at[k])
        g_copy.start()
        p_copy.start()
        loads.append((g_copy, p_copy))

    barrier = pltpu.get_barrier_semaphore()
    for axis, n, me in (("gx", nx, me_x), ("gy", ny, me_y), ("gz", nz, me_z)):
        for d in range(1, n):
            pl.semaphore_signal(
                barrier, inc=1, device_id={axis: lax.rem(me + d, n)},
                device_id_type=pl.DeviceIdType.MESH,
            )
    pl.semaphore_wait(barrier, nx + ny + nz - 3)

    ones = jnp.ones((16, columns), bf16)
    sc_z[me_z] = jnp.zeros(sc_z.shape[1:], f32)
    col_all[me_y] = jnp.zeros(col_all.shape[1:], f32)
    for l in range(layers):
        carry = (jnp.zeros((8, columns), f32), jnp.zeros((8, columns), f32))
        for c in range(chunks):
            k = l * chunks + c
            for copy in loads[k]:
                copy.wait()

            def measure(b, carry, k=k):
                col_sum, weight_sum = carry
                block = k * per + b
                here = pl.ds(pl.multiple_of(block * LANES, LANES), LANES)
                grad = g_vm[here, :].astype(f32)
                squares = grad * grad + tiny_term
                row_all[me_z, pl.ds(block, 1), :] = row_dots(ones, squares)[0:1]
                weights = p_vm[here, :]
                return col_sum + fold(squares), weight_sum + fold(weights * weights)

            carry = lax.fori_loop(0, per, measure, carry, unroll=True)
        col_all[me_y, l : l + 1, :] = jnp.sum(carry[0], axis=0, keepdims=True)
        sc_z[me_z, l : l + 1, :] = fold_lanes(jnp.sum(carry[1], axis=0, keepdims=True))
        own = slice(l * nb, (l + 1) * nb)
        row_part = (decay_rate / nz) * row_ref[own, :] + (
            (1.0 - decay_rate) / columns_all
        ) * row_all[me_z, own, :]
        sc_z[me_z, layers + l : layers + l + 1, :] = jnp.sum(row_part, axis=0, keepdims=True)

    first = exchange("gz", (row_all, sc_z), rz_s, rz_r)
    cols = exchange("gy", (col_all,), cy_s, cy_r)
    finish(first)
    sc_y[me_y] = total(sc_z)
    scalars = exchange("gy", (sc_y,), sy_s, sy_r)
    row_new = decay_rate * row_ref[...] + (1.0 - decay_rate) * (total(row_all) / columns_all)
    row_out[...] = row_new
    finish(cols)
    col_new = decay_rate * col_ref[...] + (1.0 - decay_rate) * (
        total(col_all)[0:layers] / rows_all
    )
    col_out[...] = col_new
    finish(scalars)
    sums = jnp.sum(total(sc_y), axis=1, keepdims=True)
    weight_scale = jnp.sqrt(sums[0:layers] / (rows_all * columns_all))
    row_mean = sums[layers : 2 * layers] / rows_all
    for l in range(layers):
        own = slice(l * nb, (l + 1) * nb)
        rr_out[own, :] = lax.rsqrt(row_out[own, :] / row_mean[l : l + 1])
    col_root = lax.rsqrt(col_new)

    lane_sum = jnp.zeros((1, LANES), f32)
    pick = lax.broadcasted_iota(jnp.int32, (16, columns), 0)
    for l in range(layers):
        inverse = jnp.broadcast_to(col_root[l : l + 1] * col_root[l : l + 1], (16, columns))
        top = inverse.astype(bf16).astype(f32)
        mid = (inverse - top).astype(bf16).astype(f32)
        rest = inverse - top - mid
        left = jnp.where(
            pick == 0, top, jnp.where(pick == 1, mid, jnp.where(pick == 2, rest, 0.0))
        ).astype(bf16)

        def weigh(b, acc, first_block, left=left):
            block = first_block + b
            here = pl.ds(pl.multiple_of(block * LANES, LANES), LANES)
            grad = g_vm[here, :].astype(f32)
            sums = jnp.sum(row_dots(left, grad * grad)[0:8], axis=0, keepdims=True)
            root = rr_out[pl.ds(block, 1), :]
            return acc + sums * (root * root)

        def weigh_chunk(c, acc, l=l, weigh=weigh):
            one = functools.partial(weigh, first_block=l * nb + c * per)
            return lax.fori_loop(0, per, one, acc, unroll=True)

        lane_sum = lax.fori_loop(0, chunks, weigh_chunk, lane_sum)

    up_z[me_z] = jnp.broadcast_to(lane_sum, up_z.shape[1:])
    finish(exchange("gz", (up_z,), uz_s, uz_r))
    up_y[me_y] = total(up_z)
    finish(exchange("gy", (up_y,), uy_s, uy_r))
    up_x[me_x] = total(up_y)
    finish(exchange("gx", (up_x,), ux_s, ux_r))
    update_total = jnp.sum(total(up_x)[0:1], axis=1, keepdims=True)
    entries = layers * nx * rows_all * columns_all
    clip_factor = jnp.maximum(1.0, jnp.sqrt(update_total / entries) / clip_limit)
    col_step = col_root * (weight_scale / clip_factor)
    rc_out[...] = col_step

    stores = []
    for l in range(layers):
        for c in range(chunks):
            k = l * chunks + c

            def apply(b, carry, k=k, l=l):
                block = k * per + b
                here = pl.ds(pl.multiple_of(block * LANES, LANES), LANES)
                root = jnp.broadcast_to(rr_out[pl.ds(block, 1), :], (LANES, LANES)).T
                for j in range(0, columns, LANES):
                    cut = slice(j, j + LANES)
                    applied = g_vm[here, cut].astype(f32) * root * col_step[l : l + 1, cut]
                    new_vm[here, cut] = (p_vm[here, cut] - step_share * applied).astype(bf16)
                return carry

            lax.fori_loop(0, per, apply, 0, unroll=True)
            last = k == layers * chunks - 1
            size = chunk - small if last else chunk
            part = pl.ds(k * chunk, size)
            stores.append(pltpu.make_async_copy(new_vm.at[part], big_hbm.at[part], o_sem.at[k]))
            stores[-1].start()
            if last:
                stores.append(
                    pltpu.make_async_copy(
                        new_vm.at[pl.ds(k * chunk + size, small)], small_hbm, o_sem.at[k + 1]
                    )
                )
                stores[-1].start()
    finish(stores)


def statistics(params, grads, row_state, col_state):
    layers, rows, columns = params.shape
    nx, ny, nz = (lax.axis_size(a) for a in ("gx", "gy", "gz"))
    flat = layers * rows
    nb = rows // LANES
    per = max(q for q in range(1, 9) if nb % q == 0)
    chunk = per * LANES
    small = chunk // 2
    count = layers * (rows // chunk)
    tall = -(-2 * layers // 8) * 8
    sem = lambda n: pltpu.SemaphoreType.DMA((max(n, 1),))
    vmem, anywhere = pl.BlockSpec(memory_space=pltpu.VMEM), pl.BlockSpec(memory_space=pl.ANY)
    blocks = flat // LANES
    pairs = [2 * (nz - 1), ny - 1, ny - 1, nz - 1, ny - 1, nx - 1]
    return pl.pallas_call(
        functools.partial(stats_kernel, layers, chunk, small),
        out_shape=(
            jax.ShapeDtypeStruct((blocks, LANES), f32),
            jax.ShapeDtypeStruct((layers, columns), f32),
            jax.ShapeDtypeStruct((blocks, LANES), f32),
            jax.ShapeDtypeStruct((layers, columns), f32),
            jax.ShapeDtypeStruct((flat - small, columns), bf16),
            jax.ShapeDtypeStruct((small, columns), bf16),
        ),
        in_specs=[anywhere, anywhere, vmem, vmem],
        out_specs=(vmem, vmem, vmem, vmem, anywhere, anywhere),
        scratch_shapes=[
            pltpu.VMEM((flat, columns), f32),
            pltpu.VMEM((flat, columns), bf16),
            pltpu.VMEM((flat, columns), bf16),
            pltpu.VMEM((nz, blocks, LANES), f32),
            pltpu.VMEM((ny, -(-layers // 8) * 8, columns), f32),
            pltpu.VMEM((nz, tall, LANES), f32),
            pltpu.VMEM((ny, tall, LANES), f32),
            pltpu.VMEM((nz, 8, LANES), f32),
            pltpu.VMEM((ny, 8, LANES), f32),
            pltpu.VMEM((nx, 8, LANES), f32),
            sem(count),
            sem(count),
            sem(count + 1),
        ]
        + [sem(n) for n in pairs for _ in range(2)],
        compiler_params=pltpu.CompilerParams(
            collective_id=0, has_side_effects=True, vmem_limit_bytes=60 * 1024 * 1024
        ),
        cost_estimate=pl.CostEstimate(
            flops=20 * flat * columns, bytes_accessed=8 * flat * columns, transcendentals=0
        ),
    )(
        params.reshape(flat, columns),
        grads.reshape(flat, columns),
        row_state.reshape(blocks, LANES),
        col_state,
    )


def place_kernel(n, *refs):
    out = refs[-1]
    columns = out.shape[1] // n
    for d in range(n):
        out[:, d * columns : (d + 1) * columns] = refs[d][0]


def place(gathered, held, row0, flat, block):
    n, rows, columns = gathered.shape
    start = row0 // block
    specs = [pl.BlockSpec((1, block, columns), lambda i, d=d: (d, i, 0)) for d in range(n)]
    operands, aliases = [gathered] * n, {}
    if held is not None:
        operands.append(held)
        specs.append(pl.BlockSpec(memory_space=pl.ANY))
        aliases = {n: 0}
    return pl.pallas_call(
        functools.partial(place_kernel, n),
        grid=(rows // block,),
        in_specs=specs,
        out_specs=pl.BlockSpec((block, n * columns), lambda i: (start + i, 0)),
        out_shape=jax.ShapeDtypeStruct((flat, n * columns), bf16),
        input_output_aliases=aliases,
        cost_estimate=pl.CostEstimate(
            flops=0, bytes_accessed=4 * n * rows * columns, transcendentals=0
        ),
    )(*operands)


def body(params, grads, row_state, col_state):
    layers, rows, columns = params.shape
    row_new, col_new, row_root, col_step, big, small = statistics(
        params, grads, row_state, col_state
    )
    big_all = lax.all_gather(big, "gz", axis=0)
    small_all = lax.all_gather(small, "gz", axis=0)
    row_root = row_root.reshape(layers, rows)
    applied = grads.astype(f32) * row_root[:, :, None] * col_step[:, None, :]
    new_params = params - step_share * applied
    flat, block = layers * rows, small.shape[0]
    held = place(big_all, None, 0, flat, block)
    held = place(small_all, held, big.shape[0], flat, block)
    compute = held.reshape(layers, rows, held.shape[1])
    return (new_params, row_new.reshape(layers, rows), col_new, applied, compute)


def solution(mesh):
    in_specs = (P("gx", "gy", "gz"), P("gx", "gy", "gz"), P("gx", "gy"), P("gx", "gz"))
    out_specs = (
        P("gx", "gy", "gz"),
        P("gx", "gy"),
        P("gx", "gz"),
        P("gx", "gy", "gz"),
        P("gx", "gy", None),
    )
    return jax.shard_map(body, mesh=mesh, in_specs=in_specs, out_specs=out_specs, check_vma=False)
```

profile of v0, /device:TPU:0, one launch (start us, length us, event | category | flops | bytes accessed | tf_op | source)
XLA Modules:
  0.0 623.4 jit_solution(16942841512558169879)
XLA Ops:
  7.2 0.0 all-gather.7.cloned.1.call-start
  7.2 1.5 reshape.29.row_ref
  8.7 42.9 %shard_map.83 = (f32[84,128]{1,0:T(8,128)}, f32[3,384]{1,0:T(4,128)}, f32[84,128]{1,0:T(8,128)}, f32[3,384]{1,0:T(4,128)}, bf16[10304,384]{1,0:T(8,128)(2,1)}, /*index=5*/bf16[448,384]{1,0:T(8,128)(2,1)}) custom-call(f32[10752,384]{1,0:T(8,128)} %bitcast.10, bf16[10752,384]{1,0:T(8,128)(2,1)} %bitcast.11, f32[84,128]{1,0:T(8,128)} %reshape.29.row_ref, ...), custom_call_target="tpu_custom_call" | custom-call | flops 82575360 | bytes 33030144 | tf_op jit(solution)/shard_map/pallas_call | solution.py:231
  51.6 0.0 all-gather.7.cloned.1.call-update
  51.6 0.0 all-gather.5.cloned.1.call-start
  51.7 0.7 all-gather.5.cloned.1.call-update
  52.4 0.8 mul.24
  53.2 1.4 reshape.30
  54.6 23.7 %multiply_subtract_fusion = (f32[3,3584,384]{2,1,0:T(8,128)}, f32[3,3584,384]{2,1,0:T(8,128)}) fusion(f32[3,3584,384]{2,1,0:T(8,128)} %param.4, f32[3,384]{1,0:T(4,128)} %get-tuple-element.12, f32[3,3584]{1,0:T(4,128)S(1)} %mul.24, bf16[3,3584,384]{2,1,0:T(8,128)(2,1)} %param.5), kind=kLoop, calls=%fused_computation | loop fusion | flops 20643840 | bytes 57850368 | tf_op jit(solution)/shard_map/sub | solution.py:311
  78.4 501.6 %all-gather.7.cloned.1.call-done = bf16[41216,384]{1,0:T(8,128)(2,1)} async-done(((bf16[10304,384]{1,0:T(8,128)(2,1)}), bf16[41216,384]{1,0:T(8,128)(2,1)}) %all-gather.7.cloned.1.call-update) | async-done | bytes 31653904 | tf_op jit(solution)/shard_map/all_gather | solution.py:307
  580.0 29.9 %shard_map.84.refs_4_ = bf16[10752,1536]{1,0:T(8,128)(2,1)} custom-call(bf16[4,10304,384]{2,1,0:T(8,128)(2,1)} %bitcast.5, bf16[4,10304,384]{2,1,0:T(8,128)(2,1)} %bitcast.6, bf16[4,10304,384]{2,1,0:T(8,128)(2,1)} %bitcast.7, bf16[4,10304,384]{2,1,0:T(8,128)(2,1)} %bitcast.8), custom_call_target="tpu_custom_call" | custom-call | bytes 63307776 | tf_op jit(solution)/shard_map/pallas_call | solution.py:289
  609.9 3.5 all-gather.5.cloned.1.call-done
  613.4 0.0 copy-start
  613.4 2.5 shard_map.85
  615.9 0.0 copy-done
  615.9 0.6 copy.12
Async XLA Ops:
  7.2 572.8 %all-gather.7.cloned.1.call-start = ((), (), s32[]{:S(2)}) async-start(), calls=%async_computation.1 | async-start | bytes 39567360 | tf_op jit(solution)/shard_map/all_gather | solution.py:307
  51.6 561.8 %all-gather.5.cloned.1.call-start = ((), (), s32[]{:S(2)}) async-start(), calls=%async_computation | async-start | bytes 1720320 | tf_op jit(solution)/shard_map/all_gather | solution.py:308
  613.4 2.5 copy-start
Sparse Core Ops, SparseCore 0:
  51.8 528.2 all-gather.6
  581.6 31.8 all-gather.4
where the time goes:
time: 624 us; the launch traced here: 623 us
  waiting for transfers between devices  506 us (81%)
  Pallas kernels  75.3 us (12%)
  other arithmetic  23.7 us (4%)
  between operations  14.1 us (2%)
    all_gather x1, waiting for transfers between devices, body(): big_all = lax.all_gather(big, 'gz', axis=0)  502 us
    pallas_call x1, Pallas kernels, statistics(): pl.pallas_call(functools.partial(stats_kernel, layers, chunk, small), out...  42.9 us
    pallas_call x2, Pallas kernels, place(): pl.pallas_call(functools.partial(place_kernel, n), grid=(rows // block,),...  32.4 us
    sub x1, other arithmetic, body(): new_params = params - step_share * applied  23.7 us
  transfers between devices with their start and end apart: 2, of which 2 were waited for; matrix products, arithmetic and copies ran while one was open for 4% of the time, Pallas kernels for 5%

commit v1 on v0

v1 whole, which is shorter than its diff:
```python
import functools
import jax
import jax.numpy as jnp
from jax import lax
from jax.experimental import pallas as pl
from jax.experimental.pallas import tpu as pltpu
from jax.sharding import PartitionSpec as P

decay_rate = 0.842
tiny_term = 1e-30
step_share = 0.01
clip_limit = 1.0
LANES = 128
f32, bf16 = jnp.float32, jnp.bfloat16


def fold(values):
    return jnp.sum(values.reshape(values.shape[0] // 8, 8, values.shape[1]), axis=0)


def fold_lanes(row):
    return sum(row[:, i : i + LANES] for i in range(0, row.shape[1], LANES))


def split(values):
    high = values.astype(bf16)
    return high, (values - high.astype(f32)).astype(bf16)


def row_dots(left, values):
    dims = (((1,), (1,)), ((), ()))
    high, low = split(values)
    return lax.dot_general(left, high, dims, preferred_element_type=f32) + lax.dot_general(
        left, low, dims, preferred_element_type=f32
    )


def down(row):
    return jnp.broadcast_to(row, (LANES, LANES)).T


def exchange(axis, pick, send, recv, base=0):
    n, me = lax.axis_size(axis), lax.axis_index(axis)
    copies = []
    for d in range(1, n):
        copy = pltpu.make_async_remote_copy(
            src_ref=pick(me),
            dst_ref=pick(me),
            send_sem=send.at[base + d - 1],
            recv_sem=recv.at[base + d - 1],
            device_id={axis: lax.rem(me + d, n)},
            device_id_type=pl.DeviceIdType.MESH,
        )
        copy.start()
        copies.append(copy)
    return copies


def finish(copies):
    for copy in copies:
        copy.wait()


def total(parts):
    return functools.reduce(lambda a, b: a + b, parts)


def loop(low, high, step):
    def one(k, carry):
        step(k)
        return carry

    lax.fori_loop(low, high, one, 0)


def step_kernel(
    layers, per, late,
    p_hbm, g_hbm, row_ref, col_ref,
    row_out, col_out, root_out, step_out, all_hbm, late_hbm,
    p_vm, g_vm, new_vm, row_all, col_all, mean_all, up_z, up_y, up_x, old_row, new_row, inverse,
    p_sem, g_sem, o_sem,
    rz_s, rz_r, cy_s, cy_r, my_s, my_r, uz_s, uz_r, uy_s, uy_r, ux_s, ux_r,
    right_s, right_r, left_s, left_r,
):
    flat, columns = g_vm.shape
    rows = flat // layers
    nb, chunk = rows // LANES, per * LANES
    chunks = nb // per
    count = layers * chunks
    nx, ny, nz = (lax.axis_size(a) for a in ("gx", "gy", "gz"))
    me_x, me_y, me_z = (lax.axis_index(a) for a in ("gx", "gy", "gz"))
    rows_all, columns_all = rows * ny, columns * nz

    def part(k):
        return pl.ds(pl.multiple_of(k * chunk, chunk), chunk)

    def block(b):
        return pl.ds(pl.multiple_of(b * LANES, LANES), LANES)

    def g_load(k):
        return pltpu.make_async_copy(g_hbm.at[part(k)], g_vm.at[part(k)], g_sem.at[k])

    def p_load(k):
        return pltpu.make_async_copy(p_hbm.at[part(k)], p_vm.at[part(k)], p_sem.at[k])

    loop(0, count, lambda k: g_load(k).start())
    loop(0, count, lambda k: p_load(k).start())

    barrier = pltpu.get_barrier_semaphore()
    for axis, n, me in (("gx", nx, me_x), ("gy", ny, me_y), ("gz", nz, me_z)):
        for d in range(1, n):
            pl.semaphore_signal(
                barrier, inc=1, device_id={axis: lax.rem(me + d, n)},
                device_id_type=pl.DeviceIdType.MESH,
            )

    for l in range(layers):
        for b in range(nb):
            old_row[l, b : b + 1, :] = row_ref[l : l + 1, b * LANES : (b + 1) * LANES]
        if row_all.shape[2] > nb:
            row_all[me_z, l, nb:, :] = jnp.zeros((row_all.shape[2] - nb, LANES), f32)
    up_z[me_z] = jnp.zeros(up_z.shape[1:], f32)
    pl.semaphore_wait(barrier, nx + ny + nz - 3)

    ones = jnp.ones((16, LANES), bf16)
    first = []
    for l in range(layers):

        def measure_chunk(c, col_sum, l=l):
            k = l * chunks + c
            g_load(k).wait()

            def measure(b, col_sum):
                grad = g_vm[block(k * per + b), :].astype(f32)
                squares = grad * grad
                row_all[me_z, l, pl.ds(c * per + b, 1), :] = row_dots(ones, fold_lanes(squares))[0:1]
                return col_sum + fold(squares)

            return lax.fori_loop(0, per, measure, col_sum, unroll=True)

        col_all[me_y, l] = lax.fori_loop(0, chunks, measure_chunk, jnp.zeros((8, columns), f32))
        first.append(
            exchange("gz", lambda me, l=l: row_all.at[me, l], rz_s, rz_r, l * (nz - 1))
            + exchange("gy", lambda me, l=l: col_all.at[me, l], cy_s, cy_r, l * (ny - 1))
        )

    def weigh_params(l):
        def weigh_chunk(c, acc):
            k = l * chunks + c
            p_load(k).wait()

            def one(b, acc):
                weights = p_vm[block(k * per + b), :]
                return acc + fold(fold_lanes(weights * weights))

            return lax.fori_loop(0, per, one, acc, unroll=True)

        acc = lax.fori_loop(0, chunks, weigh_chunk, jnp.zeros((8, LANES), f32))
        up_z[me_z, 1 + l : 2 + l, :] = jnp.sum(acc, axis=0, keepdims=True)

    for l in range(layers - 1):
        weigh_params(l)

    means, lane_sums = [], []
    for l in range(layers):
        finish(first[l])
        row_mean_sq = total([row_all[z, l, 0:nb, :] for z in range(nz)]) / columns_all + tiny_term
        row_now = decay_rate * old_row[l, 0:nb, :] + (1.0 - decay_rate) * row_mean_sq
        new_row[l, 0:nb, :] = row_now
        inverse[l, 0:nb, :] = 1.0 / row_now
        mean_all[me_y, l] = jnp.broadcast_to(jnp.sum(row_now, axis=0, keepdims=True), (8, LANES))
        means += exchange("gy", lambda me, l=l: mean_all.at[me, l], my_s, my_r, l * (ny - 1))
        col_sum = jnp.sum(total([col_all[y, l] for y in range(ny)]), axis=0, keepdims=True)
        col_now = decay_rate * col_ref[l : l + 1, :] + (1.0 - decay_rate) * (
            col_sum / rows_all + tiny_term
        )
        col_out[l : l + 1, :] = col_now
        inverse_col = 1.0 / col_now

        def weigh_chunk(c, acc, l=l, inverse_col=inverse_col):
            def weigh(b, acc):
                grad = g_vm[block((l * chunks + c) * per + b), :].astype(f32)
                share = fold_lanes(grad * grad * inverse_col)
                return acc + fold(share * down(inverse[l, pl.ds(c * per + b, 1), :]))

            return lax.fori_loop(0, per, weigh, acc, unroll=True)

        lane_sums.append(lax.fori_loop(0, chunks, weigh_chunk, jnp.zeros((8, LANES), f32)))

    weigh_params(layers - 1)
    finish(means)
    row_means = []
    for l in range(layers):
        row_sum = total([mean_all[y, l, 0:1, :] for y in range(ny)])
        row_means.append(jnp.sum(row_sum, axis=1, keepdims=True) / rows_all)
    up_z[me_z, 0:1, :] = total(
        [jnp.sum(lane_sums[l], axis=0, keepdims=True) * row_means[l] for l in range(layers)]
    )

    copies = exchange("gz", lambda me: up_z.at[me], uz_s, uz_r)
    for l in range(layers):
        inverse[l, 0:nb, :] = lax.rsqrt(new_row[l, 0:nb, :] / row_means[l])
    finish(copies)
    up_y[me_y] = total([up_z[z] for z in range(nz)])
    finish(exchange("gy", lambda me: up_y.at[me], uy_s, uy_r))
    up_x[me_x] = total([up_y[y] for y in range(ny)])
    copies = exchange("gx", lambda me: up_x.at[me], ux_s, ux_r)
    weight_sums = jnp.sum(up_x[me_x, 1 : 1 + layers, :], axis=1, keepdims=True)
    scaled = lax.rsqrt(col_out[...]) * jnp.sqrt(weight_sums / (rows_all * columns_all))
    finish(copies)
    update_total = jnp.sum(total([up_x[x, 0:1, :] for x in range(nx)]), axis=1, keepdims=True)
    entries = layers * nx * rows_all * columns_all
    clip_factor = jnp.maximum(1.0, jnp.sqrt(update_total / entries) / clip_limit)
    col_step = scaled / clip_factor
    step_out[...] = col_step

    sides = ((1, me_z, right_s, right_r), (-1, nz - 1 - me_z, left_s, left_r))

    def late_part(k):
        return pl.ds(pl.multiple_of((k - (count - late)) * chunk, chunk), chunk)

    def hop(side, s, k, to_late=False):
        way, _, send, recv = side
        shard = me_z - way * (s - 1)
        slot = (s - 1) * count + k
        target = late_hbm.at[late_part(k)] if to_late else all_hbm.at[shard, part(k)]
        return pltpu.make_async_remote_copy(
            src_ref=new_vm.at[part(k)] if s == 1 else all_hbm.at[shard, part(k)],
            dst_ref=target,
            send_sem=send.at[slot],
            recv_sem=recv.at[slot],
            device_id={"gz": me_z + way},
            device_id_type=pl.DeviceIdType.MESH,
        )

    def arrival(side, s, k):
        way, _, send, recv = side
        slot = (s - 1) * count + k
        here = all_hbm.at[me_z - way * s, part(k)]
        return pltpu.make_async_remote_copy(
            src_ref=here,
            dst_ref=here,
            send_sem=send.at[slot],
            recv_sem=recv.at[slot],
            device_id={"gz": me_z + way},
            device_id_type=pl.DeviceIdType.MESH,
        )

    def for_hop(side, s, k, is_late, act):
        place = side[1]
        if s == nz - 1 and is_late:
            return
        if s == nz - 2 and is_late:

            @pl.when(place == nz - 3)
            def _():
                act(hop(side, s, k, True))

            @pl.when(place == nz - 2)
            def _():
                act(hop(side, s, k))

        else:

            @pl.when(jnp.logical_and(place >= s - 1, place < nz - 1))
            def _():
                act(hop(side, s, k))

    def own(k):
        return pltpu.make_async_copy(new_vm.at[part(k)], all_hbm.at[me_z, part(k)], o_sem.at[k])

    def launch(k):
        for side in sides:
            for_hop(side, 1, k, False, lambda copy: copy.start())
        own(k).start()

    less = col_step * step_share
    for l in range(layers):

        def apply_chunk(c, l=l):
            k = l * chunks + c

            def apply(b, carry):
                here = block(k * per + b)
                root = down(inverse[l, pl.ds(c * per + b, 1), :])
                for j in range(0, columns, LANES):
                    cut = slice(j, j + LANES)
                    taken = g_vm[here, cut].astype(f32) * root * less[l : l + 1, cut]
                    new_vm[here, cut] = (p_vm[here, cut] - taken).astype(bf16)
                return carry

            lax.fori_loop(0, per, apply, 0, unroll=True)
            pl.when(k > 0)(lambda: launch(k - 1))

        loop(0, chunks, apply_chunk)
    launch(count - 1)

    for l in range(layers):
        for b in range(nb):
            cut = slice(b * LANES, (b + 1) * LANES)
            row_out[l : l + 1, cut] = new_row[l, b : b + 1, :]
            root_out[l : l + 1, cut] = inverse[l, b : b + 1, :]

    for s in range(1, nz):
        for low, high, is_late in ((0, count - late, False), (count - late, count, True)):
            if s == nz - 1 and is_late:
                continue

            def pass_on(k, s=s, is_late=is_late):
                for side in sides:
                    pl.when(side[1] >= s)(lambda side=side: arrival(side, s, k).wait_recv())
                    if s + 1 < nz:
                        for_hop(side, s + 1, k, is_late, lambda copy: copy.start())

            loop(low, high, pass_on)

    for s in range(1, nz):
        for low, high, is_late in ((0, count - late, False), (count - late, count, True)):

            def sent(k, s=s, is_late=is_late):
                for side in sides:
                    for_hop(side, s, k, is_late, lambda copy: copy.wait_send())

            loop(low, high, sent)
    loop(0, count, lambda k: own(k).wait())


def cuts(layers, rows):
    nb = rows // LANES
    per = max(q for q in range(1, 9) if nb % q == 0)
    count = layers * (nb // per)
    return per, count, max(1, count // 3)


def step(params, grads, row_state, col_state):
    layers, rows, columns = params.shape
    nx, ny, nz = (lax.axis_size(a) for a in ("gx", "gy", "gz"))
    assert nz > 3
    flat = layers * rows
    nb = rows // LANES
    per, count, late = cuts(layers, rows)
    padded = -(-nb // 8) * 8
    tall = -(-(1 + layers) // 8) * 8
    sem = lambda n: pltpu.SemaphoreType.DMA((max(n, 1),))
    vmem, anywhere = pl.BlockSpec(memory_space=pltpu.VMEM), pl.BlockSpec(memory_space=pl.ANY)
    pairs = [layers * (nz - 1), layers * (ny - 1), layers * (ny - 1), nz - 1, ny - 1, nx - 1]
    pairs += [(nz - 1) * count] * 2
    return pl.pallas_call(
        functools.partial(step_kernel, layers, per, late),
        out_shape=(
            jax.ShapeDtypeStruct((layers, rows), f32),
            jax.ShapeDtypeStruct((layers, columns), f32),
            jax.ShapeDtypeStruct((layers, rows), f32),
            jax.ShapeDtypeStruct((layers, columns), f32),
            jax.ShapeDtypeStruct((nz, flat, columns), bf16),
            jax.ShapeDtypeStruct((late * per * LANES, columns), bf16),
        ),
        in_specs=[anywhere, anywhere, vmem, vmem],
        out_specs=(vmem, vmem, vmem, vmem, anywhere, anywhere),
        scratch_shapes=[
            pltpu.VMEM((flat, columns), f32),
            pltpu.VMEM((flat, columns), bf16),
            pltpu.VMEM((flat, columns), bf16),
            pltpu.VMEM((nz, layers, padded, LANES), f32),
            pltpu.VMEM((ny, layers, 8, columns), f32),
            pltpu.VMEM((ny, layers, 8, LANES), f32),
            pltpu.VMEM((nz, tall, LANES), f32),
            pltpu.VMEM((ny, tall, LANES), f32),
            pltpu.VMEM((nx, tall, LANES), f32),
            pltpu.VMEM((layers, padded, LANES), f32),
            pltpu.VMEM((layers, padded, LANES), f32),
            pltpu.VMEM((layers, padded, LANES), f32),
            sem(count),
            sem(count),
            sem(count),
        ]
        + [sem(n) for n in pairs for _ in range(2)],
        compiler_params=pltpu.CompilerParams(
            collective_id=0, has_side_effects=True, vmem_limit_bytes=60 * 1024 * 1024
        ),
        cost_estimate=pl.CostEstimate(
            flops=20 * flat * columns, bytes_accessed=8 * flat * columns, transcendentals=0
        ),
    )(params.reshape(flat, columns), grads.reshape(flat, columns), row_state, col_state)


def place_kernel(late_chunks, chunk, from_hbm, out_hbm, stage, in_sem, out_sem):
    n, flat, columns = from_hbm.shape
    count, me = flat // chunk, lax.axis_index("gz")

    def copies(d, k):
        part = pl.ds(pl.multiple_of(k * chunk, chunk), chunk)
        slot = d * count + k
        return (
            pltpu.make_async_copy(from_hbm.at[d, part], stage.at[d, part], in_sem.at[slot]),
            pltpu.make_async_copy(
                stage.at[d, part], out_hbm.at[part, pl.ds(d * columns, columns)], out_sem.at[slot]
            ),
        )

    def whole(act):
        for d in range(n):
            missing = me < 2 if d == n - 1 else me > n - 3 if d == 0 else None
            loop(0, count - late_chunks, lambda k, d=d: act(*copies(d, k)))
            rest = lambda d=d: loop(count - late_chunks, count, lambda k: act(*copies(d, k)))
            if missing is None:
                rest()
            else:
                pl.when(jnp.logical_not(missing))(rest)

    def relay(take, put):
        take.wait()
        put.start()

    whole(lambda take, put: take.start())
    whole(relay)
    whole(lambda take, put: put.wait())


def place(gathered, late_chunks, chunk):
    n, flat, columns = gathered.shape
    anywhere = pl.BlockSpec(memory_space=pl.ANY)
    slots = n * (flat // chunk)
    return pl.pallas_call(
        functools.partial(place_kernel, late_chunks, chunk),
        in_specs=[anywhere],
        out_specs=anywhere,
        out_shape=jax.ShapeDtypeStruct((flat, n * columns), bf16),
        scratch_shapes=[
            pltpu.VMEM((n, flat, columns), bf16),
            pltpu.SemaphoreType.DMA((slots,)),
            pltpu.SemaphoreType.DMA((slots,)),
        ],
        compiler_params=pltpu.CompilerParams(vmem_limit_bytes=60 * 1024 * 1024),
        cost_estimate=pl.CostEstimate(
            flops=n * flat * columns, bytes_accessed=4 * n * flat * columns, transcendentals=0
        ),
    )(gathered)


def place_late_kernel(n, chunk, held_hbm, late_hbm, moved_hbm, out_hbm, stage, in_sem, out_sem):
    rows, columns = late_hbm.shape
    count, me = rows // chunk, lax.axis_index("gz")
    start = out_hbm.shape[0] - rows

    def move(source, d):
        def copies(k):
            part = pl.ds(k * chunk, chunk)
            there = pl.ds(start + k * chunk, chunk)
            return (
                pltpu.make_async_copy(source.at[part], stage.at[part], in_sem.at[k]),
                pltpu.make_async_copy(
                    stage.at[part], out_hbm.at[there, pl.ds(d * columns, columns)], out_sem.at[k]
                ),
            )

        both = [copies(k) for k in range(count)]
        for take, _ in both:
            take.start()
        for take, put in both:
            take.wait()
            put.start()
        for _, put in both:
            put.wait()

    for at, source, d in (
        (0, moved_hbm, n - 1), (1, late_hbm, n - 1), (n - 2, late_hbm, 0), (n - 1, moved_hbm, 0)
    ):
        pl.when(me == at)(lambda source=source, d=d: move(source, d))


def place_late(held, late, moved, n, chunk):
    anywhere = pl.BlockSpec(memory_space=pl.ANY)
    rows, columns = late.shape
    return pl.pallas_call(
        functools.partial(place_late_kernel, n, chunk),
        in_specs=[anywhere] * 3,
        out_specs=anywhere,
        out_shape=jax.ShapeDtypeStruct(held.shape, bf16),
        scratch_shapes=[
            pltpu.VMEM((rows, columns), bf16),
            pltpu.SemaphoreType.DMA((rows // chunk,)),
            pltpu.SemaphoreType.DMA((rows // chunk,)),
        ],
        input_output_aliases={0: 0},
        cost_estimate=pl.CostEstimate(
            flops=rows * columns, bytes_accessed=4 * rows * columns, transcendentals=0
        ),
    )(held, late, moved)


def body(params, grads, row_state, col_state):
    layers, rows, columns = params.shape
    n = lax.axis_size("gz")
    per, count, late_chunks = cuts(layers, rows)
    row_new, col_new, row_root, col_step, gathered, late = step(
        params, grads, row_state, col_state
    )
    moved = lax.ppermute(late, "gz", [(n - 2, n - 1), (1, 0)])
    applied = grads.astype(f32) * row_root[:, :, None] * col_step[:, None, :]
    new_params = params - step_share * applied
    held = place(gathered, late_chunks, per * LANES)
    held = place_late(held, late, moved, n, per * LANES)
    compute = held.reshape(layers, rows, n * columns)
    return (new_params, row_new, col_new, applied, compute)


def solution(mesh):
    in_specs = (P("gx", "gy", "gz"), P("gx", "gy", "gz"), P("gx", "gy"), P("gx", "gz"))
    out_specs = (
        P("gx", "gy", "gz"),
        P("gx", "gy"),
        P("gx", "gz"),
        P("gx", "gy", "gz"),
        P("gx", "gy", None),
    )
    return jax.shard_map(body, mesh=mesh, in_specs=in_specs, out_specs=out_specs, check_vma=False)
```

time: 624 us -> 570 us (0.913)
  waiting for transfers between devices: 506 us -> 19.3 us
  Pallas kernels: 75.3 us -> 524 us
  between operations: 14.1 us -> 0.71 us
    all_gather x2 -> x0, waiting for transfers between devices: 505 us -> none  [the longest x1 502 us: body(): big_all = lax.all_gather(big, 'gz', axis=0)]
    pallas_call x3, Pallas kernels: 75.3 us -> 524 us  [the longest x1 501 us: step(): pl.pallas_call(functools.partial(step_kernel, layers, per, late), out_sha...]
    ppermute x0 -> x1, waiting for transfers between devices: none -> 19.3 us  [body(): moved = lax.ppermute(late, 'gz', [(n - 2, n - 1), (1, 0)])]
  transfers between devices with their start and end apart: 2 -> 1, of which waited for: 2 -> 1; matrix products, arithmetic and copies ran while one was open for 4% -> 4% of each run, Pallas kernels for 5% -> 4%
where the time goes in v1:
time: 570 us; the launch traced here: 569 us
  Pallas kernels  524 us (92%)
  other arithmetic  21.1 us (4%)
  waiting for transfers between devices  19.3 us (3%)
    pallas_call x1, Pallas kernels, step(): pl.pallas_call(functools.partial(step_kernel, layers, per, late), out_sha...  501 us
    sub x1, other arithmetic, body(): new_params = params - step_share * applied  21.1 us
    pallas_call x1, Pallas kernels, place(): pl.pallas_call(functools.partial(place_kernel, late_chunks, chunk), in_sp...  20.8 us
    ppermute x1, waiting for transfers between devices, body(): moved = lax.ppermute(late, 'gz', [(n - 2, n - 1), (1, 0)])  19.3 us
  transfers between devices with their start and end apart: 1, of which 1 were waited for; matrix products, arithmetic and copies ran while one was open for 4% of the time, Pallas kernels for 4%

profile of v1, /device:TPU:0, one launch (start us, length us, event | category | flops | bytes accessed | tf_op | source)
XLA Modules:
  0.0 569.5 jit_solution(752897432067615192)
XLA Ops:
  0.6 500.8 %shard_map.83 = (f32[3,3584]{1,0:T(4,128)}, f32[3,384]{1,0:T(4,128)}, f32[3,3584]{1,0:T(4,128)}, f32[3,384]{1,0:T(4,128)}, bf16[4,10752,384]{2,1,0:T(8,128)(2,1)}, /*index=5*/bf16[3584,384]{1,0:T(8,128)(2,1)}) custom-call(f32[10752,384]{1,0:T(8,128)} %bitcast.4, bf16[10752,384]{1,0:T(8,128)(2,1)} %bitcast.5, f32[3,3584]{1,0:T(4,128)} %row_ref.1, ...), custom_call_target="tpu_custom_call" | custom-call | flops 82575360 | bytes 33030144 | tf_op jit(solution)/shard_map/pallas_call | solution.py:348
  501.4 1.3 collective-permute-start
  502.7 0.0 copy-start.1
  502.7 0.0 copy-start.3
  502.7 20.8 %shard_map.84.held_hbm = bf16[10752,1536]{1,0:T(8,128)(2,1)} custom-call(bf16[4,10752,384]{2,1,0:T(8,128)(2,1)} %get-tuple-element.15.from_hbm), custom_call_target="tpu_custom_call" | custom-call | flops 16515072 | bytes 66060288 | tf_op jit(solution)/shard_map/pallas_call | solution.py:424
  523.6 0.0 copy-done.1
  523.6 0.0 copy-done.3
  523.6 21.1 %multiply_subtract_fusion = (f32[3,3584,384]{2,1,0:T(8,128)}, f32[3,3584,384]{2,1,0:T(8,128)}) fusion(f32[3,3584,384]{2,1,0:T(8,128)} %param.4, f32[3,384]{1,0:T(4,128)S(1)} %copy-done.3, f32[3,3584]{1,0:T(4,128)S(1)} %copy-done.1, bf16[3,3584,384]{2,1,0:T(8,128)(2,1)} %param.5), kind=kLoop, calls=%fused_computation | loop fusion | flops 20643840 | bytes 57850368 | tf_op jit(solution)/shard_map/sub | solution.py:501
  544.7 0.0 copy-start.2
  544.7 0.0 copy-start.4
  544.7 19.3 %collective-permute-done.moved_hbm = bf16[3584,384]{1,0:T(8,128)(2,1)S(1)} collective-permute-done((bf16[3584,384]{1,0:T(8,128)(2,1)}, bf16[3584,384]{1,0:T(8,128)(2,1)S(1)}, u32[]{:S(2)}, u32[]{:S(2)}) %collective-permute-start) | collective-permute-done | bytes 2752544 | tf_op jit(solution)/shard_map/ppermute | solution.py:499
  564.0 0.0 copy-start
  564.0 1.5 copy-done
  565.5 2.7 shard_map.85
  568.2 0.0 copy-done.2
  568.2 0.6 copy.13
  568.9 0.0 copy-done.4
  568.9 0.6 copy.14
Async XLA Ops:
  501.4 62.6 %collective-permute-start = (bf16[3584,384]{1,0:T(8,128)(2,1)}, bf16[3584,384]{1,0:T(8,128)(2,1)S(1)}, u32[]{:S(2)}, u32[]{:S(2)}) collective-permute-start(bf16[3584,384]{1,0:T(8,128)(2,1)} %get-tuple-element.16.late_hbm), channel_id=1, source_target_pairs={{2,3},{1,0},{6,7},{5,4},{10,11},{9,8},{14,15},{13,12},{18,19},{17,... | collective-permute-start | bytes 8257544 | tf_op jit(solution)/shard_map/ppermute | solution.py:499
  502.7 20.8 %copy-start.1 = (f32[3,3584]{1,0:T(4,128)S(1)}, f32[3,3584]{1,0:T(4,128)}, u32[]{:S(2)}) copy-start(f32[3,3584]{1,0:T(4,128)} %get-tuple-element.11) | copy-start | bytes 129028
  502.7 20.8 %copy-start.3 = (f32[3,384]{1,0:T(4,128)S(1)}, f32[3,384]{1,0:T(4,128)}, u32[]{:S(2)}) copy-start(f32[3,384]{1,0:T(4,128)} %get-tuple-element.12) | copy-start | bytes 13828
  544.7 23.5 %copy-start.2 = (f32[3,3584]{1,0:T(4,128)S(1)}, f32[3,3584]{1,0:T(4,128)}, u32[]{:S(2)}) copy-start(f32[3,3584]{1,0:T(4,128)} %get-tuple-element.25) | copy-start | bytes 129028
  544.7 24.2 %copy-start.4 = (f32[3,384]{1,0:T(4,128)S(1)}, f32[3,384]{1,0:T(4,128)}, u32[]{:S(2)}) copy-start(f32[3,384]{1,0:T(4,128)} %get-tuple-element.26) | copy-start | bytes 13828
  564.0 1.5 copy-start

commit v2 on v1

v2 whole, which is shorter than its diff:
```python
import functools
import itertools
import jax
import jax.numpy as jnp
from jax import lax
from jax.experimental import pallas as pl
from jax.experimental.pallas import tpu as pltpu
from jax.sharding import PartitionSpec as P

decay_rate = 0.842
tiny_term = 1e-30
step_share = 0.01
clip_limit = 1.0
LANES = 128
f32, bf16 = jnp.float32, jnp.bfloat16


def fold(values):
    return jnp.sum(values.reshape(values.shape[0] // 8, 8, values.shape[1]), axis=0)


def fold_lanes(row):
    return sum(row[:, i : i + LANES] for i in range(0, row.shape[1], LANES))


def down(row):
    return jnp.broadcast_to(row, (LANES, LANES)).T


def peers(axes):
    mine = [lax.axis_index(a) for a in axes]
    sizes = [lax.axis_size(a) for a in axes]
    for shift in itertools.product(*[range(n) for n in sizes]):
        if any(shift):
            yield {a: lax.rem(m + d, n) for a, m, d, n in zip(axes, mine, shift, sizes)}


def exchange(axes, mine, send, recv, base, act):
    for slot, device in enumerate(peers(axes)):
        act(
            pltpu.make_async_remote_copy(
                src_ref=mine,
                dst_ref=mine,
                send_sem=send.at[base + slot],
                recv_sem=recv.at[base + slot],
                device_id=device,
                device_id_type=pl.DeviceIdType.MESH,
            )
        )


def start(copy):
    copy.start()


def finish(copy):
    copy.wait()


def total(parts):
    return functools.reduce(lambda a, b: a + b, parts)


def loop(low, high, step):
    def one(k, carry):
        step(k)
        return carry

    lax.fori_loop(low, high, one, 0)


def step_kernel(
    layers, per, late, early,
    p_hbm, g_hbm, row_hbm, col_hbm,
    row_out, col_out, root_out, step_out, all_hbm, late_hbm,
    p_vm, g_vm, new_vm, row_vm, root_vm, old_col, col_vm, step_vm,
    row_all, col_all, sum_all, up_all, new_row, inverse, root,
    near_p, near_g, near_col, near_new,
    p_sem, g_sem, o_sem, small_in, small_out, near_s, near_r, near_o,
    rz_s, rz_r, cy_s, cy_r, sum_s, sum_r, up_s, up_r,
    right_s, right_r, left_s, left_r,
):
    flat, columns = g_vm.shape
    rows = flat // layers
    nb, chunk = rows // LANES, per * LANES
    chunks = nb // per
    count = layers * chunks
    nx, ny, nz = (lax.axis_size(a) for a in ("gx", "gy", "gz"))
    me_x, me_y, me_z = (lax.axis_index(a) for a in ("gx", "gy", "gz"))
    rows_all, columns_all = rows * ny, columns * nz

    def part(k):
        return pl.ds(pl.multiple_of(k * chunk, chunk), chunk)

    def block(b):
        return pl.ds(pl.multiple_of(b * LANES, LANES), LANES)

    def g_load(k):
        return pltpu.make_async_copy(g_hbm.at[part(k)], g_vm.at[part(k)], g_sem.at[k])

    def p_load(k):
        return pltpu.make_async_copy(p_hbm.at[part(k)], p_vm.at[part(k)], p_sem.at[k])

    sides = ((1, me_z, right_s, right_r), (-1, nz - 1 - me_z, left_s, left_r))

    loop(0, count, lambda k: g_load(k).start())
    olds = [
        pltpu.make_async_copy(row_hbm, row_vm, small_in.at[0]),
        pltpu.make_async_copy(col_hbm, old_col, small_in.at[1]),
    ]
    for copy in olds:
        copy.start()
    loop(0, count, lambda k: p_load(k).start())

    plane = ("gy", "gz")
    barrier = pltpu.get_barrier_semaphore()
    for device in itertools.chain(peers(plane), peers(("gx",))):
        pl.semaphore_signal(
            barrier, inc=1, device_id=device, device_id_type=pl.DeviceIdType.MESH
        )

    if per < 8:

        def clear(k):
            row_all[me_z, k, per:, :] = jnp.zeros((8 - per, LANES), f32)

        loop(0, count, clear)

    def rows_of(k, act):
        exchange(("gz",), row_all.at[me_z, k], rz_s, rz_r, k * (nz - 1), act)

    def columns_of(l, act):
        exchange(("gy",), col_all.at[me_y, l], cy_s, cy_r, l * (ny - 1), act)

    for l in range(layers):

        def measure_chunk(c, col_sum, l=l):
            k = l * chunks + c
            g_load(k).wait()
            for b in range(per):
                grad = g_vm[block(k * per + b), :].astype(f32)
                squares = grad * grad
                row_all[me_z, k, b : b + 1, :] = jnp.sum(
                    fold_lanes(squares).T, axis=0, keepdims=True
                )
                col_sum = col_sum + fold(squares)
            if l > 0:
                rows_of(k, start)
            return col_sum

        col_all[me_y, l] = lax.fori_loop(0, chunks, measure_chunk, jnp.zeros((8, columns), f32))
        if l == 0:
            pl.semaphore_wait(barrier, ny * nz + nx - 2)
            loop(0, chunks, lambda c: rows_of(c, start))
        columns_of(l, start)

    for copy in olds:
        copy.wait()
    for l in range(layers):
        for b in range(nb):
            new_row[l * chunks + b // per, b % per : b % per + 1, :] = row_vm[
                l : l + 1, b * LANES : (b + 1) * LANES
            ]

    packed = jnp.zeros((2, LANES), f32)
    lane = lax.broadcasted_iota(jnp.int32, (2, LANES), 1)
    line = lax.broadcasted_iota(jnp.int32, (2, LANES), 0)

    def pack(packed, at_line, at_lane, values):
        value = jnp.sum(jnp.sum(values, axis=0, keepdims=True), axis=1, keepdims=True)
        return jnp.where(jnp.logical_and(line == at_line, lane == at_lane), value, packed)

    for l in range(layers):

        def params_chunk(c, acc, l=l):
            k = l * chunks + c
            p_load(k).wait()
            for b in range(per):
                weights = p_vm[block(k * per + b), :]
                acc = acc + fold(fold_lanes(weights * weights))
            return acc

        params_sum = lax.fori_loop(0, chunks, params_chunk, jnp.zeros((8, LANES), f32))

        columns_of(l, finish)
        col_sum = jnp.sum(total([col_all[y, l] for y in range(ny)]), axis=0, keepdims=True)
        col_now = decay_rate * old_col[l : l + 1, :] + (1.0 - decay_rate) * (
            col_sum / rows_all + tiny_term
        )
        col_vm[l : l + 1, :] = col_now
        inverse_col = 1.0 / col_now

        def weigh_chunk(c, carry, l=l, inverse_col=inverse_col):
            acc, row_sum = carry
            k = l * chunks + c
            rows_of(k, finish)
            squares = total([row_all[z, k, 0:per, :] for z in range(nz)]) / columns_all + tiny_term
            row_now = decay_rate * new_row[k, 0:per, :] + (1.0 - decay_rate) * squares
            new_row[k, 0:per, :] = row_now
            inverse[k, 0:per, :] = 1.0 / row_now
            root[k, 0:per, :] = lax.rsqrt(row_now)
            for b in range(per):
                grad = g_vm[block(k * per + b), :].astype(f32)
                share = fold_lanes(grad * grad * inverse_col)
                acc = acc + fold(share * down(inverse[k, b : b + 1, :]))
            return acc, row_sum + row_now

        acc, row_sum = lax.fori_loop(
            0, chunks, weigh_chunk, (jnp.zeros((8, LANES), f32), jnp.zeros((per, LANES), f32))
        )
        packed = pack(packed, 0, l, acc)
        packed = pack(packed, 1, l, row_sum)
        packed = pack(packed, 0, layers + l, params_sum)

    sum_all[me_y, me_z] = packed
    exchange(plane, sum_all.at[me_y, me_z], sum_s, sum_r, 0, start)

    last = pl.ds(flat - early, early)

    def near(side, act):
        for i, (source, target) in enumerate(
            ((col_vm, near_col), (p_hbm.at[last], near_p), (g_hbm.at[last], near_g))
        ):
            act(
                pltpu.make_async_remote_copy(
                    src_ref=source,
                    dst_ref=target,
                    send_sem=near_s.at[i],
                    recv_sem=near_r.at[i],
                    device_id={"gz": me_z + side[0]},
                    device_id_type=pl.DeviceIdType.MESH,
                )
            )

    for side in sides:
        pl.when(side[1] == nz - 2)(lambda side=side: near(side, start))
    col_root = lax.rsqrt(col_vm[...])
    exchange(plane, sum_all.at[me_y, me_z], sum_s, sum_r, 0, finish)
    here = total([sum_all[y, z] for y in range(ny) for z in range(nz)])
    both = jnp.where(lane[0:1] < layers, here[0:1] * here[1:2], 0.0)
    up_all[me_x] = jnp.broadcast_to(both, (2, LANES))
    exchange(("gx",), up_all.at[me_x], up_s, up_r, 0, start)
    parts, scales = [], []
    for l in range(layers):
        row_mean = here[1:2, l : l + 1] / (nz * rows_all)
        weight_scale = jnp.sqrt(here[0:1, layers + l : layers + l + 1] / (rows_all * columns_all))
        scales.append(jnp.sqrt(row_mean) * weight_scale)
        parts.append(col_root[l : l + 1] * scales[l])
    exchange(("gx",), up_all.at[me_x], up_s, up_r, 0, finish)
    update_sum = total([up_all[x, 0:1] for x in range(nx)])
    update_total = jnp.sum(update_sum, axis=1, keepdims=True) / (nz * rows_all)
    entries = layers * nx * rows_all * columns_all
    clip_factor = jnp.maximum(1.0, jnp.sqrt(update_total / entries) / clip_limit)
    for l in range(layers):
        step_vm[l : l + 1, :] = parts[l] / clip_factor
    less = step_vm[...] * step_share

    def late_part(k):
        return pl.ds(pl.multiple_of((k - (count - late)) * chunk, chunk), chunk)

    def size_of(k, short):
        return pl.ds(pl.multiple_of(k * chunk, chunk), chunk - early) if short else part(k)

    def hop(side, s, k, to_late=False, short=False):
        way, _, send, recv = side
        shard = me_z - way * (s - 1)
        slot = (s - 1) * count + k
        rows_k = size_of(k, short)
        target = late_hbm.at[late_part(k)] if to_late else all_hbm.at[shard, rows_k]
        return pltpu.make_async_remote_copy(
            src_ref=new_vm.at[rows_k] if s == 1 else all_hbm.at[shard, rows_k],
            dst_ref=target,
            send_sem=send.at[slot],
            recv_sem=recv.at[slot],
            device_id={"gz": me_z + way},
            device_id_type=pl.DeviceIdType.MESH,
        )

    def arrival(side, s, k, short=False):
        way, _, send, recv = side
        slot = (s - 1) * count + k
        here = all_hbm.at[me_z - way * s, size_of(k, short)]
        return pltpu.make_async_remote_copy(
            src_ref=here,
            dst_ref=here,
            send_sem=send.at[slot],
            recv_sem=recv.at[slot],
            device_id={"gz": me_z + way},
            device_id_type=pl.DeviceIdType.MESH,
        )

    def for_arrival(side, s, k, final):
        if final:
            pl.when(side[1] == nz - 1)(lambda: arrival(side, s, k, True).wait_recv())
            full = jnp.logical_and(side[1] >= s, side[1] < nz - 1)
        else:
            full = side[1] >= s
        pl.when(full)(lambda: arrival(side, s, k).wait_recv())

    def for_hop(side, s, k, is_late, act, final=False):
        place = side[1]
        if s == nz - 1 and is_late:
            return
        if s == nz - 2 and is_late:

            @pl.when(place == nz - 3)
            def _():
                act(hop(side, s, k, True))

            @pl.when(place == nz - 2)
            def _():
                act(hop(side, s, k))

        elif final:

            @pl.when(place < nz - 2)
            def _():
                act(hop(side, s, k))

            @pl.when(place == nz - 2)
            def _():
                act(hop(side, s, k, short=True))

        else:

            @pl.when(jnp.logical_and(place >= s - 1, place < nz - 1))
            def _():
                act(hop(side, s, k))

    def own(k):
        return pltpu.make_async_copy(new_vm.at[part(k)], all_hbm.at[me_z, part(k)], o_sem.at[k])

    def launch(k, final=False):
        for side in sides:
            for_hop(side, 1, k, False, start, final)
        own(k).start()

    for l in range(layers):

        def apply_chunk(c, l=l):
            k = l * chunks + c

            for b in range(per):
                here = block(k * per + b)
                factor = down(root[k, b : b + 1, :])
                for j in range(0, columns, LANES):
                    cut = slice(j, j + LANES)
                    taken = g_vm[here, cut].astype(f32) * factor * less[l : l + 1, cut]
                    new_vm[here, cut] = (p_vm[here, cut] - taken).astype(bf16)

            pl.when(k > 0)(lambda: launch(k - 1))

        loop(0, chunks, apply_chunk)
    launch(count - 1, True)

    def near_rows(side):
        near(side, lambda copy: copy.wait_recv())
        l, k = layers - 1, count - 1
        near_less = lax.rsqrt(near_col[l : l + 1, :]) * scales[l] / clip_factor * step_share
        skip = chunk - early
        for b in range(skip // LANES, per):
            low = max(0, skip - b * LANES)
            rows_b = slice(b * LANES + low - skip, (b + 1) * LANES - skip)
            factor = down(root[k, b : b + 1, :])[low:, :]
            for j in range(0, columns, LANES):
                cut = slice(j, j + LANES)
                taken = near_g[rows_b, cut].astype(f32) * factor * near_less[:, cut]
                near_new[rows_b, cut] = (near_p[rows_b, cut] - taken).astype(bf16)

    def near_put(side):
        return pltpu.make_async_copy(near_new, all_hbm.at[me_z - side[0], last], near_o)

    for side in sides:
        pl.when(side[1] == nz - 1)(lambda side=side: near_rows(side))
        pl.when(side[1] == nz - 2)(lambda side=side: near(side, lambda copy: copy.wait_send()))

    for l in range(layers):
        for b in range(nb):
            cut = slice(b * LANES, (b + 1) * LANES)
            k, i = l * chunks + b // per, b % per
            row_vm[l : l + 1, cut] = new_row[k, i : i + 1, :]
            root_vm[l : l + 1, cut] = root[k, i : i + 1, :]
    smalls = [
        pltpu.make_async_copy(source, target, small_out.at[i])
        for i, (source, target) in enumerate(
            ((row_vm, row_out), (col_vm, col_out), (root_vm, root_out), (step_vm, step_out))
        )
    ]
    for copy in smalls:
        copy.start()

    for side in sides:
        pl.when(side[1] == nz - 1)(lambda side=side: near_put(side).start())

    def pass_on(s, k, is_late, final=False):
        for side in sides:
            for_arrival(side, s, k, final)
            if s + 1 < nz:
                for_hop(side, s + 1, k, is_late, start)
        for side in sides:
            for_hop(side, s, k, is_late, lambda copy: copy.wait_send(), final)

    for s in range(1, nz):
        if s == nz - 1:
            loop(0, count, lambda k: own(k).wait())
            for copy in smalls:
                copy.wait()
            for side in sides:
                pl.when(side[1] == nz - 1)(lambda side=side: near_put(side).wait())
        loop(0, count - late, lambda k, s=s: pass_on(s, k, False))
        if s == 1:
            loop(count - late, count - 1, lambda k: pass_on(1, k, True))
            pass_on(1, count - 1, True, True)
        elif s < nz - 1:
            loop(count - late, count, lambda k, s=s: pass_on(s, k, True))


def cuts(layers, rows):
    nb = rows // LANES
    per = max(q for q in range(1, 9) if nb % q == 0)
    count = layers * (nb // per)
    return per, count, max(1, count // 3), min(192, (per - 1) * LANES)


def step(params, grads, row_state, col_state):
    layers, rows, columns = params.shape
    nx, ny, nz = (lax.axis_size(a) for a in ("gx", "gy", "gz"))
    assert nz > 3
    flat = layers * rows
    per, count, late, early = cuts(layers, rows)
    sem = lambda n: pltpu.SemaphoreType.DMA((max(n, 1),))
    anywhere = pl.BlockSpec(memory_space=pl.ANY)
    pairs = [count * (nz - 1), layers * (ny - 1), ny * nz - 1, nx - 1] + [(nz - 1) * count] * 2
    return pl.pallas_call(
        functools.partial(step_kernel, layers, per, late, early),
        out_shape=(
            jax.ShapeDtypeStruct((layers, rows), f32),
            jax.ShapeDtypeStruct((layers, columns), f32),
            jax.ShapeDtypeStruct((layers, rows), f32),
            jax.ShapeDtypeStruct((layers, columns), f32),
            jax.ShapeDtypeStruct((nz, flat, columns), bf16),
            jax.ShapeDtypeStruct((late * per * LANES, columns), bf16),
        ),
        in_specs=[anywhere] * 4,
        out_specs=(anywhere,) * 6,
        scratch_shapes=[
            pltpu.VMEM((flat, columns), f32),
            pltpu.VMEM((flat, columns), bf16),
            pltpu.VMEM((flat, columns), bf16),
            pltpu.VMEM((layers, rows), f32),
            pltpu.VMEM((layers, rows), f32),
            pltpu.VMEM((layers, columns), f32),
            pltpu.VMEM((layers, columns), f32),
            pltpu.VMEM((layers, columns), f32),
            pltpu.VMEM((nz, count, 8, LANES), f32),
            pltpu.VMEM((ny, layers, 8, columns), f32),
            pltpu.VMEM((ny, nz, 2, LANES), f32),
            pltpu.VMEM((nx, 2, LANES), f32),
            pltpu.VMEM((count, 8, LANES), f32),
            pltpu.VMEM((count, 8, LANES), f32),
            pltpu.VMEM((count, 8, LANES), f32),
            pltpu.VMEM((early, columns), f32),
            pltpu.VMEM((early, columns), bf16),
            pltpu.VMEM((layers, columns), f32),
            pltpu.VMEM((early, columns), bf16),
            sem(count),
            sem(count),
            sem(count),
            sem(2),
            sem(4),
            sem(3),
            sem(3),
            pltpu.SemaphoreType.DMA,
        ]
        + [sem(n) for n in pairs for _ in range(2)],
        compiler_params=pltpu.CompilerParams(
            collective_id=0, has_side_effects=True, vmem_limit_bytes=60 * 1024 * 1024
        ),
        cost_estimate=pl.CostEstimate(
            flops=20 * flat * columns, bytes_accessed=8 * flat * columns, transcendentals=0
        ),
    )(params.reshape(flat, columns), grads.reshape(flat, columns), row_state, col_state)


def place_kernel(
    late_chunks, chunk, from_hbm, late_hbm, row_in, col_in,
    out_hbm, row_out, col_out, stage, in_sem, out_sem,
):
    n, flat, columns = from_hbm.shape
    count, me = flat // chunk, lax.axis_index("gz")
    main = count - late_chunks
    row_out[...] = row_in[...]
    col_out[...] = col_in[...]

    def part(k):
        return pl.ds(pl.multiple_of(k * chunk, chunk), chunk)

    def copies(d, k, source):
        slot = d * count + k
        return (
            pltpu.make_async_copy(source, stage.at[d, part(k)], in_sem.at[slot]),
            pltpu.make_async_copy(
                stage.at[d, part(k)],
                out_hbm.at[part(k), pl.ds(d * columns, columns)],
                out_sem.at[slot],
            ),
        )

    def whole(act):
        for d in range(n):
            usual = lambda k, d=d: act(*copies(d, k, from_hbm.at[d, part(k)]))
            aside = lambda k, d=d: act(*copies(d, k, late_hbm.at[part(k - main)]))
            loop(0, main, usual)
            away = n - 1 - me if d == n - 1 else me if d == 0 else None
            if away is None:
                loop(main, count, usual)
            else:
                pl.when(away < n - 2)(lambda usual=usual: loop(main, count, usual))
                pl.when(away == n - 2)(lambda aside=aside: loop(main, count, aside))

    def relay(take, put):
        take.wait()
        put.start()

    whole(lambda take, put: take.start())
    whole(relay)
    whole(lambda take, put: put.wait())


def place(gathered, late, row_new, col_new, late_chunks, chunk):
    n, flat, columns = gathered.shape
    hbm, vmem = pl.BlockSpec(memory_space=pltpu.HBM), pl.BlockSpec(memory_space=pltpu.VMEM)
    slots = n * (flat // chunk)
    return pl.pallas_call(
        functools.partial(place_kernel, late_chunks, chunk),
        in_specs=[hbm, hbm, vmem, vmem],
        out_specs=(hbm, vmem, vmem),
        out_shape=(
            jax.ShapeDtypeStruct((flat, n * columns), bf16),
            jax.ShapeDtypeStruct(row_new.shape, f32),
            jax.ShapeDtypeStruct(col_new.shape, f32),
        ),
        scratch_shapes=[
            pltpu.VMEM((n, flat, columns), bf16),
            pltpu.SemaphoreType.DMA((slots,)),
            pltpu.SemaphoreType.DMA((slots,)),
        ],
        compiler_params=pltpu.CompilerParams(vmem_limit_bytes=56 * 1024 * 1024),
        cost_estimate=pl.CostEstimate(
            flops=n * flat * columns, bytes_accessed=4 * n * flat * columns, transcendentals=0
        ),
    )(gathered, late, row_new, col_new)


def place_late_kernel(n, held_hbm, moved, out_hbm, sem):
    rows, columns = moved.shape
    there = pl.ds(out_hbm.shape[0] - rows, rows)
    for at, d in ((0, n - 1), (n - 1, 0)):

        @pl.when(lax.axis_index("gz") == at)
        def _(d=d):
            target = out_hbm.at[there, pl.ds(d * columns, columns)]
            copy = pltpu.make_async_copy(moved, target, sem)
            copy.start()
            copy.wait()


def place_late(held, moved, n):
    anywhere = pl.BlockSpec(memory_space=pl.ANY)
    rows, columns = moved.shape
    return pl.pallas_call(
        functools.partial(place_late_kernel, n),
        in_specs=[anywhere, pl.BlockSpec(memory_space=pltpu.VMEM)],
        out_specs=anywhere,
        out_shape=jax.ShapeDtypeStruct(held.shape, bf16),
        scratch_shapes=[pltpu.SemaphoreType.DMA],
        input_output_aliases={0: 0},
        compiler_params=pltpu.CompilerParams(vmem_limit_bytes=8 * 1024 * 1024),
        cost_estimate=pl.CostEstimate(
            flops=rows * columns, bytes_accessed=4 * rows * columns, transcendentals=0
        ),
    )(held, moved)


def body(params, grads, row_state, col_state):
    layers, rows, columns = params.shape
    n = lax.axis_size("gz")
    per, count, late_chunks, _ = cuts(layers, rows)
    row_new, col_new, row_root, col_step, gathered, late = step(
        params, grads, row_state, col_state
    )
    moved = lax.ppermute(late, "gz", [(n - 2, n - 1), (1, 0)])
    applied = grads.astype(f32) * row_root[:, :, None] * col_step[:, None, :]
    new_params = params - step_share * applied
    held, row_new, col_new = place(gathered, late, row_new, col_new, late_chunks, per * LANES)
    held = place_late(held, moved, n)
    compute = held.reshape(layers, rows, n * columns)
    return (new_params, row_new, col_new, applied, compute)


def solution(mesh):
    in_specs = (P("gx", "gy", "gz"), P("gx", "gy", "gz"), P("gx", "gy"), P("gx", "gz"))
    out_specs = (
        P("gx", "gy", "gz"),
        P("gx", "gy"),
        P("gx", "gz"),
        P("gx", "gy", "gz"),
        P("gx", "gy", None),
    )
    return jax.shard_map(body, mesh=mesh, in_specs=in_specs, out_specs=out_specs, check_vma=False)
```

time: 570 us -> 559 us (0.981)
    pallas_call x2, Pallas kernels: 503 us -> 496 us  [the longest x1 495 us: step(): pl.pallas_call(functools.partial(step_kernel, layers, per, late, early),...]
where the time goes in v2:
time: 559 us
  Pallas kernels  519 us (93%)
  other arithmetic  21.1 us (4%)
  waiting for transfers between devices  17.6 us (3%)
    pallas_call x1, Pallas kernels, step(): pl.pallas_call(functools.partial(step_kernel, layers, per, late, early),...  495 us
    pallas_call x1, Pallas kernels, place(): pl.pallas_call(functools.partial(place_kernel, late_chunks, chunk), in_sp...  22.3 us
    sub x1, other arithmetic, body(): new_params = params - step_share * applied  21.1 us
    ppermute x1, waiting for transfers between devices, body(): moved = lax.ppermute(late, 'gz', [(n - 2, n - 1), (1, 0)])  17.6 us
  transfers between devices with their start and end apart: 1, of which 1 were waited for; matrix products, arithmetic and copies ran while one was open for 4% of the time, Pallas kernels for 4%

profile of v2, /device:TPU:0, one launch (start us, length us, event | category | flops | bytes accessed | tf_op | source)
XLA Modules:
  0.0 559.2 jit_solution(7128324253200393845)
XLA Ops:
  0.6 494.7 %shard_map.83 = (f32[3,3584]{1,0:T(4,128)}, f32[3,384]{1,0:T(4,128)}, f32[3,3584]{1,0:T(4,128)}, f32[3,384]{1,0:T(4,128)}, bf16[4,10752,384]{2,1,0:T(8,128)(2,1)}, /*index=5*/bf16[3584,384]{1,0:T(8,128)(2,1)}) custom-call(f32[10752,384]{1,0:T(8,128)} %bitcast.3, bf16[10752,384]{1,0:T(8,128)(2,1)} %bitcast.4, f32[3,3584]{1,0:T(4,128)} %row_hbm.1, ...), custom_call_target="tpu_custom_call" | custom-call | flops 82575360 | bytes 33030144 | tf_op jit(solution)/shard_map/pallas_call | solution.py:434
  495.4 1.3 collective-permute-start
  496.7 0.0 copy-start
  496.7 0.0 copy-start.1
  496.7 22.3 %shard_map.84 = (bf16[10752,1536]{1,0:T(8,128)(2,1)}, f32[3,3584]{1,0:T(4,128)}, f32[3,384]{1,0:T(4,128)}) custom-call(bf16[4,10752,384]{2,1,0:T(8,128)(2,1)} %get-tuple-element.16.from_hbm, bf16[3584,384]{1,0:T(8,128)(2,1)} %get-tuple-element.17.late_hbm, f32[3,3584]{1,0:T(4,128)} %get-tuple-element.18.row_in, f32[3,384]{1,0:T(4,128)} %get-tuple-element.19.col_in), custom_call_target="tpu_custom_call" | custom-call | flops 16515072 | bytes 66060288 | tf_op jit(solution)/shard_map/pallas_call | solution.py:534
  519.0 0.0 copy-done
  519.0 0.0 copy-done.1
  519.0 21.1 %multiply_subtract_fusion = (f32[3,3584,384]{2,1,0:T(8,128)}, f32[3,3584,384]{2,1,0:T(8,128)}) fusion(f32[3,3584,384]{2,1,0:T(8,128)} %param.4, f32[3,384]{1,0:T(4,128)S(1)} %copy-done.1, f32[3,3584]{1,0:T(4,128)S(1)} %copy-done, bf16[3,3584,384]{2,1,0:T(8,128)(2,1)} %param.5), kind=kLoop, calls=%fused_computation | loop fusion | flops 20643840 | bytes 57850368 | tf_op jit(solution)/shard_map/sub | solution.py:594
  540.1 17.6 %collective-permute-done.moved = bf16[3584,384]{1,0:T(8,128)(2,1)S(1)} collective-permute-done((bf16[3584,384]{1,0:T(8,128)(2,1)}, bf16[3584,384]{1,0:T(8,128)(2,1)S(1)}, u32[]{:S(2)}, u32[]{:S(2)}) %collective-permute-start) | collective-permute-done | bytes 2752544 | tf_op jit(solution)/shard_map/ppermute | solution.py:592
  557.7 1.5 shard_map.85
Async XLA Ops:
  495.4 62.3 %collective-permute-start = (bf16[3584,384]{1,0:T(8,128)(2,1)}, bf16[3584,384]{1,0:T(8,128)(2,1)S(1)}, u32[]{:S(2)}, u32[]{:S(2)}) collective-permute-start(bf16[3584,384]{1,0:T(8,128)(2,1)} %get-tuple-element.17.late_hbm), channel_id=1, source_target_pairs={{2,3},{1,0},{6,7},{5,4},{10,11},{9,8},{14,15},{13,12},{18,19},{17,... | collective-permute-start | bytes 8257544 | tf_op jit(solution)/shard_map/ppermute | solution.py:592
  496.7 22.3 %copy-start = (f32[3,3584]{1,0:T(4,128)S(1)}, f32[3,3584]{1,0:T(4,128)}, u32[]{:S(2)}) copy-start(f32[3,3584]{1,0:T(4,128)} %get-tuple-element.14) | copy-start | bytes 129028
  496.7 22.3 %copy-start.1 = (f32[3,384]{1,0:T(4,128)S(1)}, f32[3,384]{1,0:T(4,128)}, u32[]{:S(2)}) copy-start(f32[3,384]{1,0:T(4,128)} %get-tuple-element.15) | copy-start | bytes 13828

commit v3 on v2

--- a/solution.py
+++ b/solution.py
@@ -74,10 +74,10 @@
     p_hbm, g_hbm, row_hbm, col_hbm,
     row_out, col_out, root_out, step_out, all_hbm, late_hbm,
     p_vm, g_vm, new_vm, row_vm, root_vm, old_col, col_vm, step_vm,
-    row_all, col_all, sum_all, up_all, new_row, inverse, root,
+    row_all, col_all, sum_all, up_all, param_all, new_row, inverse, root,
     near_p, near_g, near_col, near_new,
     p_sem, g_sem, o_sem, small_in, small_out, near_s, near_r, near_o,
-    rz_s, rz_r, cy_s, cy_r, sum_s, sum_r, up_s, up_r,
+    rz_s, rz_r, cy_s, cy_r, sum_s, sum_r, up_s, up_r, param_s, param_r,
     right_s, right_r, left_s, left_r,
 ):
     flat, columns = g_vm.shape
@@ -154,6 +154,36 @@
             loop(0, chunks, lambda c: rows_of(c, start))
         columns_of(l, start)
 
+    last = pl.ds(flat - early, early)
+    first_rows = early // 48 * 16
+
+    def near(side, act, which=(0, 1, 2, 3, 4)):
+        head = pl.ds(flat - early, first_rows)
+        rest = pl.ds(flat - early + first_rows, early - first_rows)
+        head_to, rest_to = pl.ds(0, first_rows), pl.ds(first_rows, early - first_rows)
+        moves = (
+            (col_vm, near_col),
+            (p_hbm.at[head], near_p.at[head_to]),
+            (g_hbm.at[head], near_g.at[head_to]),
+            (p_hbm.at[rest], near_p.at[rest_to]),
+            (g_hbm.at[rest], near_g.at[rest_to]),
+        )
+        for i in which:
+            source, target = moves[i]
+            act(
+                pltpu.make_async_remote_copy(
+                    src_ref=source,
+                    dst_ref=target,
+                    send_sem=near_s.at[i],
+                    recv_sem=near_r.at[i],
+                    device_id={"gz": me_z + side[0]},
+                    device_id_type=pl.DeviceIdType.MESH,
+                )
+            )
+
+    for side in sides:
+        pl.when(side[1] == nz - 2)(lambda side=side: near(side, start, (1, 2)))
+
     for copy in olds:
         copy.wait()
     for l in range(layers):
@@ -171,16 +201,6 @@
         return jnp.where(jnp.logical_and(line == at_line, lane == at_lane), value, packed)
 
     for l in range(layers):
-
-        def params_chunk(c, acc, l=l):
-            k = l * chunks + c
-            p_load(k).wait()
-            for b in range(per):
-                weights = p_vm[block(k * per + b), :]
-                acc = acc + fold(fold_lanes(weights * weights))
-            return acc
-
-        params_sum = lax.fori_loop(0, chunks, params_chunk, jnp.zeros((8, LANES), f32))
 
         columns_of(l, finish)
         col_sum = jnp.sum(total([col_all[y, l] for y in range(ny)]), axis=0, keepdims=True)
@@ -210,40 +230,41 @@
         )
         packed = pack(packed, 0, l, acc)
         packed = pack(packed, 1, l, row_sum)
-        packed = pack(packed, 0, layers + l, params_sum)
 
     sum_all[me_y, me_z] = packed
     exchange(plane, sum_all.at[me_y, me_z], sum_s, sum_r, 0, start)
 
-    last = pl.ds(flat - early, early)
-
-    def near(side, act):
-        for i, (source, target) in enumerate(
-            ((col_vm, near_col), (p_hbm.at[last], near_p), (g_hbm.at[last], near_g))
-        ):
-            act(
-                pltpu.make_async_remote_copy(
-                    src_ref=source,
-                    dst_ref=target,
-                    send_sem=near_s.at[i],
-                    recv_sem=near_r.at[i],
-                    device_id={"gz": me_z + side[0]},
-                    device_id_type=pl.DeviceIdType.MESH,
-                )
-            )
-
+    col_root = lax.rsqrt(col_vm[...])
+
+    packed = jnp.zeros((2, LANES), f32)
+    for l in range(layers):
+
+        def params_chunk(c, acc, l=l):
+            k = l * chunks + c
+            p_load(k).wait()
+            for b in range(per):
+                weights = p_vm[block(k * per + b), :]
+                acc = acc + fold(fold_lanes(weights * weights))
+            return acc
+
+        params_sum = lax.fori_loop(0, chunks, params_chunk, jnp.zeros((8, LANES), f32))
+        packed = pack(packed, 0, l, params_sum)
+    param_all[me_y, me_z] = packed
+    exchange(plane, param_all.at[me_y, me_z], param_s, param_r, 0, start)
     for side in sides:
-        pl.when(side[1] == nz - 2)(lambda side=side: near(side, start))
-    col_root = lax.rsqrt(col_vm[...])
+        pl.when(side[1] == nz - 2)(lambda side=side: near(side, start, (0, 3, 4)))
+
     exchange(plane, sum_all.at[me_y, me_z], sum_s, sum_r, 0, finish)
     here = total([sum_all[y, z] for y in range(ny) for z in range(nz)])
     both = jnp.where(lane[0:1] < layers, here[0:1] * here[1:2], 0.0)
     up_all[me_x] = jnp.broadcast_to(both, (2, LANES))
     exchange(("gx",), up_all.at[me_x], up_s, up_r, 0, start)
+    exchange(plane, param_all.at[me_y, me_z], param_s, param_r, 0, finish)
+    params_sums = total([param_all[y, z, 0:1] for y in range(ny) for z in range(nz)])
     parts, scales = [], []
     for l in range(layers):
         row_mean = here[1:2, l : l + 1] / (nz * rows_all)
-        weight_scale = jnp.sqrt(here[0:1, layers + l : layers + l + 1] / (rows_all * columns_all))
+        weight_scale = jnp.sqrt(params_sums[:, l : l + 1] / (rows_all * columns_all))
         scales.append(jnp.sqrt(row_mean) * weight_scale)
         parts.append(col_root[l : l + 1] * scales[l])
     exchange(("gx",), up_all.at[me_x], up_s, up_r, 0, finish)
@@ -347,8 +368,8 @@
                     cut = slice(j, j + LANES)
                     taken = g_vm[here, cut].astype(f32) * factor * less[l : l + 1, cut]
                     new_vm[here, cut] = (p_vm[here, cut] - taken).astype(bf16)
-
-            pl.when(k > 0)(lambda: launch(k - 1))
+                if b == min(1, per - 1):
+                    pl.when(k > 0)(lambda: launch(k - 1))
 
         loop(0, chunks, apply_chunk)
     launch(count - 1, True)
@@ -430,7 +451,7 @@
     per, count, late, early = cuts(layers, rows)
     sem = lambda n: pltpu.SemaphoreType.DMA((max(n, 1),))
     anywhere = pl.BlockSpec(memory_space=pl.ANY)
-    pairs = [count * (nz - 1), layers * (ny - 1), ny * nz - 1, nx - 1] + [(nz - 1) * count] * 2
+    pairs = [count * (nz - 1), layers * (ny - 1), ny * nz - 1, nx - 1, ny * nz - 1] + [(nz - 1) * count] * 2
     return pl.pallas_call(
         functools.partial(step_kernel, layers, per, late, early),
         out_shape=(
@@ -456,6 +477,7 @@
             pltpu.VMEM((ny, layers, 8, columns), f32),
             pltpu.VMEM((ny, nz, 2, LANES), f32),
             pltpu.VMEM((nx, 2, LANES), f32),
+            pltpu.VMEM((ny, nz, 2, LANES), f32),
             pltpu.VMEM((count, 8, LANES), f32),
             pltpu.VMEM((count, 8, LANES), f32),
             pltpu.VMEM((count, 8, LANES), f32),
@@ -468,8 +490,8 @@
             sem(count),
             sem(2),
             sem(4),
-            sem(3),
-            sem(3),
+            sem(5),
+            sem(5),
             pltpu.SemaphoreType.DMA,
         ]
         + [sem(n) for n in pairs for _ in range(2)],

time: 559 us -> 557 us (level)
  no operation moved by 1% of the time
where the time goes in v3:
time: 557 us
  Pallas kernels  516 us (93%)
  other arithmetic  21.1 us (4%)
  waiting for transfers between devices  17.6 us (3%)
    pallas_call x1, Pallas kernels, step(): pl.pallas_call(functools.partial(step_kernel, layers, per, late, early),...  493 us
    pallas_call x1, Pallas kernels, place(): pl.pallas_call(functools.partial(place_kernel, late_chunks, chunk), in_sp...  22.3 us
    sub x1, other arithmetic, body(): new_params = params - step_share * applied  21.1 us
    ppermute x1, waiting for transfers between devices, body(): moved = lax.ppermute(late, 'gz', [(n - 2, n - 1), (1, 0)])  17.6 us
  transfers between devices with their start and end apart: 1, of which 1 were waited for; matrix products, arithmetic and copies ran while one was open for 4% of the time, Pallas kernels for 4%

profile of v3, /device:TPU:0, one launch (start us, length us, event | category | flops | bytes accessed | tf_op | source)
XLA Modules:
  0.0 557.1 jit_solution(15157845589989104428)
XLA Ops:
  0.6 492.6 %shard_map.83 = (f32[3,3584]{1,0:T(4,128)}, f32[3,384]{1,0:T(4,128)}, f32[3,3584]{1,0:T(4,128)}, f32[3,384]{1,0:T(4,128)}, bf16[4,10752,384]{2,1,0:T(8,128)(2,1)}, /*index=5*/bf16[3584,384]{1,0:T(8,128)(2,1)}) custom-call(f32[10752,384]{1,0:T(8,128)} %bitcast.3, bf16[10752,384]{1,0:T(8,128)(2,1)} %bitcast.4, f32[3,3584]{1,0:T(4,128)} %row_hbm.1, ...), custom_call_target="tpu_custom_call" | custom-call | flops 82575360 | bytes 33030144 | tf_op jit(solution)/shard_map/pallas_call | solution.py:455
  493.2 1.3 collective-permute-start
  494.5 0.0 copy-start
  494.5 0.0 copy-start.1
  494.5 22.3 %shard_map.84 = (bf16[10752,1536]{1,0:T(8,128)(2,1)}, f32[3,3584]{1,0:T(4,128)}, f32[3,384]{1,0:T(4,128)}) custom-call(bf16[4,10752,384]{2,1,0:T(8,128)(2,1)} %get-tuple-element.16.from_hbm, bf16[3584,384]{1,0:T(8,128)(2,1)} %get-tuple-element.17.late_hbm, f32[3,3584]{1,0:T(4,128)} %get-tuple-element.18.row_in, f32[3,384]{1,0:T(4,128)} %get-tuple-element.19.col_in), custom_call_target="tpu_custom_call" | custom-call | flops 16515072 | bytes 66060288 | tf_op jit(solution)/shard_map/pallas_call | solution.py:556
  516.8 0.0 copy-done
  516.8 0.0 copy-done.1
  516.8 21.1 %multiply_subtract_fusion = (f32[3,3584,384]{2,1,0:T(8,128)}, f32[3,3584,384]{2,1,0:T(8,128)}) fusion(f32[3,3584,384]{2,1,0:T(8,128)} %param.4, f32[3,384]{1,0:T(4,128)S(1)} %copy-done.1, f32[3,3584]{1,0:T(4,128)S(1)} %copy-done, bf16[3,3584,384]{2,1,0:T(8,128)(2,1)} %param.5), kind=kLoop, calls=%fused_computation | loop fusion | flops 20643840 | bytes 57850368 | tf_op jit(solution)/shard_map/sub | solution.py:616
  537.9 17.6 %collective-permute-done.moved = bf16[3584,384]{1,0:T(8,128)(2,1)S(1)} collective-permute-done((bf16[3584,384]{1,0:T(8,128)(2,1)}, bf16[3584,384]{1,0:T(8,128)(2,1)S(1)}, u32[]{:S(2)}, u32[]{:S(2)}) %collective-permute-start) | collective-permute-done | bytes 2752544 | tf_op jit(solution)/shard_map/ppermute | solution.py:614
  555.5 1.5 shard_map.85
Async XLA Ops:
  493.2 62.3 %collective-permute-start = (bf16[3584,384]{1,0:T(8,128)(2,1)}, bf16[3584,384]{1,0:T(8,128)(2,1)S(1)}, u32[]{:S(2)}, u32[]{:S(2)}) collective-permute-start(bf16[3584,384]{1,0:T(8,128)(2,1)} %get-tuple-element.17.late_hbm), channel_id=1, source_target_pairs={{2,3},{1,0},{6,7},{5,4},{10,11},{9,8},{14,15},{13,12},{18,19},{17,... | collective-permute-start | bytes 8257544 | tf_op jit(solution)/shard_map/ppermute | solution.py:614
  494.5 22.3 %copy-start = (f32[3,3584]{1,0:T(4,128)S(1)}, f32[3,3584]{1,0:T(4,128)}, u32[]{:S(2)}) copy-start(f32[3,3584]{1,0:T(4,128)} %get-tuple-element.14) | copy-start | bytes 129028
  494.5 22.3 %copy-start.1 = (f32[3,384]{1,0:T(4,128)S(1)}, f32[3,384]{1,0:T(4,128)}, u32[]{:S(2)}) copy-start(f32[3,384]{1,0:T(4,128)} %get-tuple-element.15) | copy-start | bytes 13828

commit v4 on v3

--- a/solution.py
+++ b/solution.py
@@ -440,7 +440,7 @@
     nb = rows // LANES
     per = max(q for q in range(1, 9) if nb % q == 0)
     count = layers * (nb // per)
-    return per, count, max(1, count // 3), min(192, (per - 1) * LANES)
+    return per, count, max(1, count // 4), min(192, (per - 1) * LANES)
 
 
 def step(params, grads, row_state, col_state):
@@ -576,15 +576,24 @@
 
 def place_late_kernel(n, held_hbm, moved, out_hbm, sem):
     rows, columns = moved.shape
-    there = pl.ds(out_hbm.shape[0] - rows, rows)
+    pieces = sem.shape[0]
+    size, first = rows // pieces, out_hbm.shape[0] - rows
     for at, d in ((0, n - 1), (n - 1, 0)):
 
         @pl.when(lax.axis_index("gz") == at)
         def _(d=d):
-            target = out_hbm.at[there, pl.ds(d * columns, columns)]
-            copy = pltpu.make_async_copy(moved, target, sem)
-            copy.start()
-            copy.wait()
+            copies = [
+                pltpu.make_async_copy(
+                    moved.at[pl.ds(i * size, size)],
+                    out_hbm.at[pl.ds(first + i * size, size), pl.ds(d * columns, columns)],
+                    sem.at[i],
+                )
+                for i in range(pieces)
+            ]
+            for copy in copies:
+                copy.start()
+            for copy in copies:
+                copy.wait()
 
 
 def place_late(held, moved, n):
@@ -595,7 +604,7 @@
         in_specs=[anywhere, pl.BlockSpec(memory_space=pltpu.VMEM)],
         out_specs=anywhere,
         out_shape=jax.ShapeDtypeStruct(held.shape, bf16),
-        scratch_shapes=[pltpu.SemaphoreType.DMA],
+        scratch_shapes=[pltpu.SemaphoreType.DMA((rows // LANES,))],
         input_output_aliases={0: 0},
         compiler_params=pltpu.CompilerParams(vmem_limit_bytes=8 * 1024 * 1024),
         cost_estimate=pl.CostEstimate(

time: 557 us -> 557 us (level)
  Pallas kernels: 516 us -> 532 us
  waiting for transfers between devices: 17.6 us -> 2.34 us
    ppermute x1, waiting for transfers between devices: 17.6 us -> 2.34 us  [body(): moved = lax.ppermute(late, 'gz', [(n - 2, n - 1), (1, 0)])]
    pallas_call x1, Pallas kernels: 493 us -> 507 us  [step(): pl.pallas_call(functools.partial(step_kernel, layers, per, late, early),...]
where the time goes in v4:
time: 557 us
  Pallas kernels  532 us (96%)
  other arithmetic  21.1 us (4%)
    pallas_call x1, Pallas kernels, step(): pl.pallas_call(functools.partial(step_kernel, layers, per, late, early),...  507 us
    pallas_call x1, Pallas kernels, place(): pl.pallas_call(functools.partial(place_kernel, late_chunks, chunk), in_sp...  22.8 us
    sub x1, other arithmetic, body(): new_params = params - step_share * applied  21.1 us
  transfers between devices with their start and end apart: 1, of which 1 were waited for; matrix products, arithmetic and copies ran while one was open for 4% of the time, Pallas kernels for 4%

profile of v4, /device:TPU:0, one launch (start us, length us, event | category | flops | bytes accessed | tf_op | source)
XLA Modules:
  0.0 557.0 jit_solution(17060051320417536930)
XLA Ops:
  0.6 507.3 %shard_map.83 = (f32[3,3584]{1,0:T(4,128)}, f32[3,384]{1,0:T(4,128)}, f32[3,3584]{1,0:T(4,128)}, f32[3,384]{1,0:T(4,128)}, bf16[4,10752,384]{2,1,0:T(8,128)(2,1)}, /*index=5*/bf16[2688,384]{1,0:T(8,128)(2,1)}) custom-call(f32[10752,384]{1,0:T(8,128)} %bitcast.3, bf16[10752,384]{1,0:T(8,128)(2,1)} %bitcast.4, f32[3,3584]{1,0:T(4,128)} %row_hbm.1, ...), custom_call_target="tpu_custom_call" | custom-call | flops 82575360 | bytes 33030144 | tf_op jit(solution)/shard_map/pallas_call | solution.py:455
  507.9 1.3 collective-permute-start
  509.2 0.0 copy-start
  509.2 0.0 copy-start.1
  509.3 22.8 %shard_map.84 = (bf16[10752,1536]{1,0:T(8,128)(2,1)}, f32[3,3584]{1,0:T(4,128)}, f32[3,384]{1,0:T(4,128)}) custom-call(bf16[4,10752,384]{2,1,0:T(8,128)(2,1)} %get-tuple-element.16.from_hbm, bf16[2688,384]{1,0:T(8,128)(2,1)} %get-tuple-element.17.late_hbm, f32[3,3584]{1,0:T(4,128)} %get-tuple-element.18.row_in, f32[3,384]{1,0:T(4,128)} %get-tuple-element.19.col_in), custom_call_target="tpu_custom_call" | custom-call | flops 16515072 | bytes 66060288 | tf_op jit(solution)/shard_map/pallas_call | solution.py:556
  532.1 0.0 copy-done
  532.1 0.0 copy-done.1
  532.1 21.1 %multiply_subtract_fusion = (f32[3,3584,384]{2,1,0:T(8,128)}, f32[3,3584,384]{2,1,0:T(8,128)}) fusion(f32[3,3584,384]{2,1,0:T(8,128)} %param.4, f32[3,384]{1,0:T(4,128)S(1)} %copy-done.1, f32[3,3584]{1,0:T(4,128)S(1)} %copy-done, bf16[3,3584,384]{2,1,0:T(8,128)(2,1)} %param.5), kind=kLoop, calls=%fused_computation | loop fusion | flops 20643840 | bytes 57850368 | tf_op jit(solution)/shard_map/sub | solution.py:625
  553.2 2.3 collective-permute-done.moved
  555.5 1.5 shard_map.85
Async XLA Ops:
  507.9 47.6 %collective-permute-start = (bf16[2688,384]{1,0:T(8,128)(2,1)}, bf16[2688,384]{1,0:T(8,128)(2,1)S(1)}, u32[]{:S(2)}, u32[]{:S(2)}) collective-permute-start(bf16[2688,384]{1,0:T(8,128)(2,1)} %get-tuple-element.17.late_hbm), channel_id=1, source_target_pairs={{2,3},{1,0},{6,7},{5,4},{10,11},{9,8},{14,15},{13,12},{18,19},{17,... | collective-permute-start | bytes 6193160 | tf_op jit(solution)/shard_map/ppermute | solution.py:623
  509.2 22.8 %copy-start = (f32[3,3584]{1,0:T(4,128)S(1)}, f32[3,3584]{1,0:T(4,128)}, u32[]{:S(2)}) copy-start(f32[3,3584]{1,0:T(4,128)} %get-tuple-element.14) | copy-start | bytes 129028
  509.2 22.8 %copy-start.1 = (f32[3,384]{1,0:T(4,128)S(1)}, f32[3,384]{1,0:T(4,128)}, u32[]{:S(2)}) copy-start(f32[3,384]{1,0:T(4,128)} %get-tuple-element.15) | copy-start | bytes 13828
